TPU v7x, 32 devices: a whole 2x2x4 slice. The times are simulated.
32 devices in a mesh: gx: 2 (over x), gy: 4 (over z), gz: 4 (over y, core).
Axes of the slice: x: 2, y: 2, z: 4, core: 2. Of those that a mesh axis runs over, the one named last changes fastest.
Arguments:
- particle_mass: float32 [1048576], P(('gx', 'gy', 'gz')), may hold values from 0.5 to 2
- particle_velocity: float32 [3, 1048576], P(None, ('gx', 'gy', 'gz')), may hold values from -6 to 6
- particle_affine: float32 [9, 1048576], P(None, ('gx', 'gy', 'gz')), may hold values from -6 to 6
- particle_cell: int32 [3, 1048576], P(None, ('gx', 'gy', 'gz')), may hold values from 0 to 13
- particle_fraction: int32 [3, 1048576], P(None, ('gx', 'gy', 'gz')), may hold values from 0 to 1023
- block_owner: int32 [2048, 1], P(('gx', 'gy', 'gz')), may hold values from 0 to 15; in each aligned block of 64 rows (0 to 63, 64 to 127, ...) at most 8 rows name the same one
- block_slot: int32 [2048], P(('gx', 'gy', 'gz')), may hold values from 0 to 31
- block_count: int32 [2048], P(('gx', 'gy', 'gz')), may hold values from 128 to 512
- cell_drag: float32 [1024, 4096], P(('gx', 'gy', 'gz')), may hold values from 0.5 to 2
Outputs:
- grid_velocity: float32 [1024, 3, 4096], P(('gx', 'gy', 'gz'))
- new_velocity: float32 [3, 1048576], P(None, ('gx', 'gy', 'gz'))
- new_affine: float32 [9, 1048576], P(None, ('gx', 'gy', 'gz'))
Inputs may be any that keep to these rules, and one draw needn't show every extreme that they name: `block_owner`: owner index counted over the devices with the particle device's own gx index, in gy+gz order; among the rows of one device, no owner is named more than 8 times. `block_count`: slots at or beyond the count are absent. `particle_cell`: A particle's three stencil nodes lie inside its grid block.
All inputs are finite; a program needn't handle non-finite values.
Results may differ from a plain program's by a relative error of at most 0.0085.
Values may be sent and summed in bfloat16 or wider, within the bound.
A program may use at most 128 MiB of HBM per device.

v0:
```python
import jax
import jax.numpy as jnp
from jax import lax
from jax.sharding import PartitionSpec as P

EDGE = 16
QUANT = 1024
batch_blocks = 4


def spline(offset):
    magnitude = jnp.abs(offset)
    inner_part = 0.75 - magnitude * magnitude
    outer_part = 0.5 * (1.5 - magnitude) * (1.5 - magnitude)
    return jnp.where(magnitude < 0.5, inner_part, jnp.where(magnitude < 1.5, outer_part, 0.0))


def particle_table(
    particle_mass, particle_velocity, particle_affine, particle_cell, particle_fraction, block_count
):
    blocks = block_count.shape[0]
    batch_shape = (blocks, particle_mass.shape[0] // blocks)
    places = jnp.arange(batch_shape[1], dtype=jnp.int32)
    present = places[None, :] < block_count[:, None]
    live_mass = jnp.where(present, particle_mass.reshape(batch_shape), 0.0)
    position = (
        particle_cell.astype(jnp.float32)
        + 0.5
        + (particle_fraction.astype(jnp.float32) + 0.5) / QUANT
    )
    return jnp.concatenate(
        [
            live_mass[None],
            particle_velocity.reshape((3,) + batch_shape),
            particle_affine.reshape((9,) + batch_shape),
            position.reshape((3,) + batch_shape),
        ],
        axis=0,
    )


def stencil(particle_data):
    node_coords = jnp.arange(EDGE, dtype=jnp.float32)
    offset = node_coords[None, :, None, None] - particle_data[13:16][:, None]
    weights = spline(offset)
    return (weights, weights * offset)


def planes(weights, slopes):

    def outer(first_factor, second_factor):
        product_table = first_factor[:, None] * second_factor[None, :]
        return product_table.reshape((EDGE * EDGE,) + product_table.shape[2:]).astype(jnp.bfloat16)

    return (
        outer(weights[1], weights[2]),
        outer(slopes[1], weights[2]),
        outer(weights[1], slopes[2]),
    )


def deposit(particle_data):
    batch_shape = particle_data.shape[1:]
    weights, slopes = stencil(particle_data)
    plane_zero, plane_one, plane_two = planes(weights, slopes)
    live_mass = particle_data[0]
    along_x = weights[0]
    slope_x = slopes[0]
    affine = particle_data[4:13].reshape((3, 3) + batch_shape)
    mass_lead = (live_mass[None] * along_x)[None]
    momentum_lead = live_mass[None, None] * (
        particle_data[1:4][:, None] * along_x[None] + affine[:, 0][:, None] * slope_x[None]
    )
    lead_zero = jnp.concatenate([mass_lead, momentum_lead], axis=0).astype(jnp.bfloat16)
    lead_one = (live_mass[None, None] * affine[:, 1][:, None] * along_x[None]).astype(jnp.bfloat16)
    lead_two = (live_mass[None, None] * affine[:, 2][:, None] * along_x[None]).astype(jnp.bfloat16)

    def contract(lead, plane):
        flattened = lead.reshape((-1,) + batch_shape)
        return jnp.einsum("anp,bnp->nab", flattened, plane, preferred_element_type=jnp.float32)

    count_blocks = batch_shape[0]
    dep_zero = contract(lead_zero, plane_zero).reshape(count_blocks, 4, -1)
    dep_one = contract(lead_one, plane_one).reshape(count_blocks, 3, -1)
    dep_two = contract(lead_two, plane_two).reshape(count_blocks, 3, -1)
    return jnp.concatenate([dep_zero[:, :1], dep_zero[:, 1:] + dep_one + dep_two], axis=1)


def interpolate(particle_data, grid_rows):
    batch_shape = particle_data.shape[1:]
    weights, slopes = stencil(particle_data)
    plane_zero, plane_one, plane_two = planes(weights, slopes)
    along_x = weights[0]
    slope_x = slopes[0]
    flattened = grid_rows.reshape(batch_shape[0], 3 * EDGE, EDGE * EDGE)

    def contract(plane):
        moment = jnp.einsum("nab,bnp->anp", flattened, plane, preferred_element_type=jnp.float32)
        return moment.reshape((3, EDGE) + batch_shape)

    moment_zero = contract(plane_zero)
    moment_one = contract(plane_one)
    moment_two = contract(plane_two)
    velocity_out = jnp.sum(along_x[None] * moment_zero, axis=1)
    column_zero = 4.0 * jnp.sum(slope_x[None] * moment_zero, axis=1)
    column_one = 4.0 * jnp.sum(along_x[None] * moment_one, axis=1)
    column_two = 4.0 * jnp.sum(along_x[None] * moment_two, axis=1)
    affine_out = jnp.stack([column_zero, column_one, column_two], axis=1).reshape(
        (9,) + batch_shape
    )
    present = (particle_data[0] > 0.0).astype(jnp.float32)
    return jnp.concatenate([velocity_out, affine_out], axis=0) * present[None]


def deposit_all(particle_data):
    block_total = particle_data.shape[1]

    def deposit_advance(state_carry, step_index):
        portion = lax.dynamic_slice_in_dim(
            particle_data, step_index * batch_blocks, batch_blocks, 1
        )
        return (state_carry, deposit(portion))

    unused, stacked = lax.scan(
        deposit_advance,
        jnp.zeros((), jnp.float32),
        jnp.arange(block_total // batch_blocks, dtype=jnp.int32),
    )
    return stacked.reshape((block_total,) + stacked.shape[2:])


def interpolate_all(particle_data, grid_rows):
    block_total = particle_data.shape[1]

    def interpolate_advance(step_index, result):
        first_block = step_index * batch_blocks
        portion = lax.dynamic_slice_in_dim(particle_data, first_block, batch_blocks, 1)
        cell_rows = lax.dynamic_slice_in_dim(grid_rows, first_block, batch_blocks, 0)
        return lax.dynamic_update_slice_in_dim(
            result, interpolate(portion, cell_rows), first_block, 1
        )

    initial = jnp.zeros((12, block_total, particle_data.shape[2]), jnp.float32)
    return lax.fori_loop(0, block_total // batch_blocks, interpolate_advance, initial)


def send_slots(owners, group_size, capacity):
    targets = jnp.arange(group_size, dtype=jnp.int32)
    matches = (owners[:, None] == targets[None, :]).astype(jnp.int32)
    earlier = jnp.cumsum(matches, axis=0) - matches
    ranking = jnp.sum(earlier * matches, axis=1)
    return owners * capacity + ranking


def slot_sources(destination, slot_count):
    positions = jnp.arange(slot_count, dtype=jnp.int32)
    matches = destination[None, :] == positions[:, None]
    block_numbers = jnp.arange(destination.shape[0], dtype=jnp.int32)
    source = jnp.sum(jnp.where(matches, block_numbers[None, :], 0), axis=1)
    return (source, jnp.any(matches, axis=1))


def match_tiles(arrived_tiles, tile_count):
    tile_numbers = jnp.arange(tile_count, dtype=jnp.float32)
    return (arrived_tiles[None, :] == tile_numbers[:, None]).astype(jnp.float32)


def update_grid(deposits, tile_match, cell_drag):
    tile_count = tile_match.shape[0]
    flattened = deposits.reshape(deposits.shape[0], -1)
    summed = jnp.dot(
        tile_match, flattened, precision=lax.Precision.HIGHEST, preferred_element_type=jnp.float32
    )
    summed = summed.reshape((tile_count,) + deposits.shape[1:])
    grid_velocity = summed[:, 1:] / (summed[:, :1] + cell_drag[:, None, :])
    rounded = grid_velocity.astype(jnp.bfloat16)
    picked = jnp.dot(
        tile_match.T.astype(jnp.bfloat16),
        rounded.reshape(tile_count, -1),
        preferred_element_type=jnp.float32,
    )
    cell_rows = picked.astype(jnp.bfloat16).reshape((deposits.shape[0], 3, -1))
    return (grid_velocity, cell_rows)


def per_device(
    particle_mass,
    particle_velocity,
    particle_affine,
    particle_cell,
    particle_fraction,
    block_owner,
    block_slot,
    block_count,
    cell_drag,
):
    group_size = lax.axis_size(("gy", "gz"))
    blocks = block_count.shape[0]
    capacity = max(1, 2 * blocks // group_size)
    slot_count = group_size * capacity
    tile_count = cell_drag.shape[0]
    particle_data = particle_table(
        particle_mass,
        particle_velocity,
        particle_affine,
        particle_cell,
        particle_fraction,
        block_count,
    )
    destination = send_slots(block_owner[:, 0], group_size, capacity)
    source, filled = slot_sources(destination, slot_count)
    tile_ids = jnp.where(filled, jnp.take(block_slot, source), -1).astype(jnp.float32)
    deposits = deposit_all(particle_data)
    outgoing = jnp.where(filled[:, None, None], jnp.take(deposits, source, axis=0), 0.0)
    arrived, arrived_tiles = (
        lax.all_to_all(outgoing, ("gy", "gz"), split_axis=0, concat_axis=0, tiled=True),
        lax.all_to_all(tile_ids, ("gy", "gz"), split_axis=0, concat_axis=0, tiled=True),
    )
    tile_match = match_tiles(arrived_tiles, tile_count)
    grid_velocity, cell_rows = update_grid(arrived, tile_match, cell_drag)
    returned = lax.all_to_all(cell_rows, ("gy", "gz"), split_axis=0, concat_axis=0, tiled=True)
    finished = interpolate_all(particle_data, jnp.take(returned, destination, axis=0))
    new_velocity = finished[:3].reshape(3, -1)
    new_affine = finished[3:].reshape(9, -1)
    return (grid_velocity, new_velocity, new_affine)


def solution(mesh):
    return jax.shard_map(
        per_device,
        mesh=mesh,
        in_specs=(
            P(("gx", "gy", "gz")),
            P(None, ("gx", "gy", "gz")),
            P(None, ("gx", "gy", "gz")),
            P(None, ("gx", "gy", "gz")),
            P(None, ("gx", "gy", "gz")),
            P(("gx", "gy", "gz"), None),
            P(("gx", "gy", "gz")),
            P(("gx", "gy", "gz")),
            P(("gx", "gy", "gz"), None),
        ),
        out_specs=(
            P(("gx", "gy", "gz"), None, None),
            P(None, ("gx", "gy", "gz")),
            P(None, ("gx", "gy", "gz")),
        ),
        check_vma=False,
    )
```

profile of v0, /device:TPU:13, one launch (start us, length us, event | category | flops | bytes accessed | tf_op | source)
XLA Modules:
  0.0 659.1 jit_solution(10529736568579550010)
XLA Ops:
  5.6 6.5 all-to-all-start
  12.2 2.8 copy.92
  18.4 167.9 %while.23 = (s32[]{:T(128)}, f32[16,4,4,4096]{3,2,1,0:T(4,128)}, s32[16]{0:T(128)S(1)}, f32[16,64,512]{2,1,0:T(8,128)}, s32[]{:T(128)}, /*index=5*/s32[]{:T(128)...) while((s32[]{:T(128)}, f32[16,4,4,4096]{3,2,1,0:T(4,128)}, s32[16]{0:T(128)S(1)}, ...), condition=%wide.region_5.6_spmd, body=%wide.region_4.5_spmd.sunk | while | flops 173355008 | bytes 15483619 | solution.py:124
  186.2 11.4 %gather_fusion.1 = f32[128,4,4096]{2,1,0:T(4,128)} fusion(f32[64,4,4096]{2,1,0:T(4,128)} %bitcast.211, s32[1024]{0:T(1024)S(1)} %pad_clamp_fusion.1), kind=kCustom, calls=%fused_computation.1 | custom fusion | bytes 16777728 | tf_op jit(solution)/shard_map/jit(_take)/gather | solution.py:214
  197.7 11.6 %select_select_fusion = f32[128,4,4096]{2,1,0:T(4,128)} fusion(f32[128,4,4096]{2,1,0:T(4,128)} %gather_fusion.1, pred[128]{0:T(512)(128)(4,1)S(1)} %compare_and_fusion, pred[128]{0:T(512)(128)(4,1)S(1)} %fusion.22), kind=kLoop, calls=%fused_computation.72 | loop fusion | flops 4194304 | bytes 16777472 | tf_op jit(solution)/shard_map/jit(_where)/select_n | solution.py:214
  209.3 6.0 all-to-all-start.1
  216.6 181.1 %all-to-all-done.1 = f32[128,4,4096]{2,1,0:T(4,128)} async-done(((f32[128,4,4096]{2,1,0:T(4,128)}), f32[128,4,4096]{2,1,0:T(4,128)}, u32[]{:S(2)}, u32[]{:S(2)}) %all-to-all-start.1) | async-done | bytes 8388640 | tf_op jit(solution)/shard_map/all_to_all | solution.py:216
  397.7 10.0 %copy.86 = f32[128,4,4096]{0,2,1:T(8,128)} copy(f32[128,4,4096]{2,1,0:T(4,128)} %all-to-all-done.1) | data formatting | bytes 16777216 | tf_op jit(solution)/shard_map/all_to_all | solution.py:216
  407.7 8.1 %fusion.17 = f32[32,4,4096]{2,0,1:T(8,128)S(1)} fusion(f32[128,4,4096]{0,2,1:T(8,128)} %copy.86, f32[128]{0:T(128)S(1)} %eq.54), kind=kOutput, calls=%fused_computation.70 | convolution fusion | flops 805310464 | bytes 10486272 | tf_op jit(solution)/shard_map/dot_general | solution.py:171
  417.3 2.7 convolution_convert_fusion
  420.0 3.5 copy.88
  423.5 5.5 copy.89
  429.0 4.9 all-to-all-start.2
  433.9 92.4 %all-to-all-done.2 = bf16[128,3,4096]{2,1,0:T(4,128)(2,1)} async-done(((bf16[128,3,4096]{2,1,0:T(4,128)(2,1)}), bf16[128,3,4096]{2,1,0:T(4,128)(2,1)}, u32[]{:S(2)}, u32[]{:S(2)}) %all-to-all-start.2) | async-done | bytes 3145760 | tf_op jit(solution)/shard_map/all_to_all | solution.py:221
  526.3 4.5 gather_fusion.2
  530.9 2.4 broadcast_select_fusion
  534.6 118.2 %while.24 = (s32[]{:T(128)}, f32[12,64,512]{2,1,0:T(8,128)}, f32[16,64,512]{2,1,0:T(8,128)}, bf16[64,3,4096]{2,1,0:T(4,128)(2,1)}, s32[]{:T(128)}, /*index=5*/s32[]{:T(128)}, s32[]{:T(128)}, s32[]{:T(128)}, s32[]{}) while((s32[]{:T(128)}, f32[12,64,512]{2,1,0:T(8,128)}, f32[16,64,512]{2,1,0:T(8,128)}, bf16[64,3,4096]{2,1,0:T(4,128)(2,1)}, ...), condition=%wide.region_11.12_spmd, body=%wide.region_6.11_spmd.sunk | while | flops 156190720 | bytes 13369515 | solution.py:144
  536.6 1.6 constant_dynamic-slice_fusion.11
  544.0 1.6 constant_dynamic-slice_fusion.11
  551.3 1.6 constant_dynamic-slice_fusion.11
  558.7 1.6 constant_dynamic-slice_fusion.11
  566.1 1.6 constant_dynamic-slice_fusion.11
  573.5 1.6 constant_dynamic-slice_fusion.11
  580.9 1.6 constant_dynamic-slice_fusion.11
  588.2 1.6 constant_dynamic-slice_fusion.11
  595.6 1.6 constant_dynamic-slice_fusion.11
  603.0 1.6 constant_dynamic-slice_fusion.11
  617.8 1.6 constant_dynamic-slice_fusion.11
  625.2 1.6 constant_dynamic-slice_fusion.11
  632.6 1.6 constant_dynamic-slice_fusion.11
  647.4 1.6 constant_dynamic-slice_fusion.11
  655.5 2.5 copy.95
  (732 shorter events, 265.7 us)
Async XLA Ops:
  0.6 2.7 copy-start
  5.6 203.7 %all-to-all-start = ((f32[16,8,1]{1,2,0:T(1,128)}), f32[16,8,1]{1,2,0:T(1,128)S(1)}, u32[]{:S(2)}, u32[]{:S(2)}) async-start(f32[16,8,1]{1,2,0:T(1,128)} %copy.85), calls=%async_computation | async-start | bytes 16384 | tf_op jit(solution)/shard_map/all_to_all | solution.py:217
  15.0 0.9 copy-start.6
  15.0 1.1 copy-start.2
  15.0 1.3 copy-start.3
  15.0 1.5 copy-start.4
  15.9 0.8 copy-start.8
  209.3 188.4 %all-to-all-start.1 = ((f32[128,4,4096]{2,1,0:T(4,128)}), f32[128,4,4096]{2,1,0:T(4,128)}, u32[]{:S(2)}, u32[]{:S(2)}) async-start(f32[128,4,4096]{2,1,0:T(4,128)} %select_select_fusion), calls=%async_computation.1 | async-start | bytes 16777216 | tf_op jit(solution)/shard_map/all_to_all | solution.py:216
  407.7 8.1 %copy-start.5 = (f32[32,4096]{1,0:T(8,128)S(1)}, f32[32,4096]{1,0:T(8,128)}, u32[]{:S(2)}) copy-start(f32[32,4096]{1,0:T(8,128)} %param.21) | copy-start | bytes 1572868
  429.0 4.9 copy-start.7
  429.0 97.4 %all-to-all-start.2 = ((bf16[128,3,4096]{2,1,0:T(4,128)(2,1)}), bf16[128,3,4096]{2,1,0:T(4,128)(2,1)}, u32[]{:S(2)}, u32[]{:S(2)}) async-start(bf16[128,3,4096]{2,1,0:T(4,128)(2,1)} %copy.89), calls=%async_computation.2 | async-start | bytes 8388608 | tf_op jit(solution)/shard_map/all_to_all | solution.py:221
  655.5 3.6 copy-start.1
where the time goes:
time: 665 us; the launch traced here: 659 us
  waiting for transfers between devices  274 us (41%)
  local copies, waits for them, and re-layouts  164 us (25%)
  other arithmetic  114 us (17%)
  matrix products  74.8 us (11%)
  starting transfers between devices  17.4 us (3%)
  loops' own time  13.9 us (2%)
    all_to_all x1, waiting for transfers between devices, per_device(): lax.all_to_all(outgoing, ('gy', 'gz'), split_axis=0, concat_axis=0, tiled...  181 us
    all_to_all x1, waiting for transfers between devices, per_device(): lax.all_to_all(cell_rows, ('gy', 'gz'), split_axis=0, concat_axis=0, tile...  92.4 us
    dot_general x48, matrix products, contract(): jnp.einsum('anp,bnp->nab', flattened, plane, preferred_element_type=jnp.f...  50.1 us
    convert_element_type x32, other arithmetic, outer(): product_table.reshape((EDGE * EDGE,) + product_table.shape[2:])  29 us
    dynamic_slice x16, local copies, waits for them, and re-layouts, interpolate_advance(): lax.dynamic_slice_in_dim(grid_rows, first_block, batch_blocks, 0)  25.8 us
    reshape x16, local copies, waits for them, and re-layouts, interpolate(): flattened = grid_rows.reshape(batch_shape[0], 3 * EDGE, EDGE * EDGE)  16.8 us
    slice x16, local copies, waits for them, and re-layouts, deposit(): affine = particle_data[4:13].reshape((3, 3) + batch_shape)  14.9 us
    another operation x32, other arithmetic  14.9 us
  transfers between devices with their start and end apart: 3, of which 2 were waited for; matrix products, arithmetic and copies ran while one was open for 28% of the time, Pallas kernels for 0%

commit v1 on v0

--- a/solution.py
+++ b/solution.py
@@ -218,7 +218,31 @@
     )
     tile_match = match_tiles(arrived_tiles, tile_count)
     grid_velocity, cell_rows = update_grid(arrived, tile_match, cell_drag)
-    returned = lax.all_to_all(cell_rows, ("gy", "gz"), split_axis=0, concat_axis=0, tiled=True)
+    carry_out = lax.psum(1, ("gy", "gz"))
+    odd = lax.axis_index(("gy", "gz"))
+    r2, step_out = (carry_out, odd)
+    current_arr = cell_rows.shape[0] // r2
+    later = list(cell_rows.shape)
+    later[0] = current_arr
+    side_arr = later[0]
+    later[0] = side_arr * r2
+    returned = jnp.zeros(later, cell_rows.dtype)
+    ix = 0
+    while ix < r2:
+        main = lax.dynamic_slice_in_dim(
+            cell_rows, (step_out ^ ix) * current_arr, current_arr, axis=0
+        )
+        if ix:
+            store = []
+            jj = 0
+            while jj < r2:
+                store.append((jj, jj ^ ix))
+                jj += 1
+            main = lax.ppermute(main, ("gy", "gz"), store)
+        returned = lax.dynamic_update_slice_in_dim(
+            returned, main, (step_out ^ ix) * side_arr, axis=0
+        )
+        ix = ix + 1
     finished = interpolate_all(particle_data, jnp.take(returned, destination, axis=0))
     new_velocity = finished[:3].reshape(3, -1)
     new_affine = finished[3:].reshape(9, -1)

time: 665 us -> 767 us (1.15); the launches traced: 659 us -> 752 us
  local copies, waits for them, and re-layouts: 164 us -> 268 us
  waiting for transfers between devices: 274 us -> 253 us
  starting transfers between devices: 17.4 us -> 26.4 us
    all_to_all x1 -> x0, waiting for transfers between devices: 92.4 us -> none  [per_device(): lax.all_to_all(cell_rows, ('gy', 'gz'), split_axis=0, concat_axis=0, tile...]
    ppermute x0 -> x15, waiting for transfers between devices: none -> 72.4 us  [per_device(): main = lax.ppermute(main, ('gy', 'gz'), store)]
    unnamed x23 -> x57, local copies, waits for them, and re-layouts: 8.83 us -> 63.9 us
    dynamic_slice x0 -> x1, local copies, waits for them, and re-layouts: none -> 20.2 us  [per_device(): lax.dynamic_slice_in_dim(cell_rows, (step_out ^ ix) * current_arr, curren...]
    dynamic_update_slice x0 -> x16, local copies, waits for them, and re-layouts: none -> 17.6 us  [per_device(): lax.dynamic_update_slice_in_dim(returned, main, (step_out ^ ix) * side_ar...]
    ppermute x0 -> x15, starting transfers between devices: none -> 13.8 us  [per_device(): main = lax.ppermute(main, ('gy', 'gz'), store)]
    gather x1, local copies, waits for them, and re-layouts: 11.4 us -> 23.3 us  [per_device(): jnp.take(deposits, source, axis=0)]
  transfers between devices with their start and end apart: 3 -> 17, of which waited for: 2 -> 9; matrix products, arithmetic and copies ran while one was open for 28% -> 35% of each run, Pallas kernels for 0% -> 0%
where the time goes in v1:
time: 767 us; the launch traced here: 752 us
  local copies, waits for them, and re-layouts  268 us (35%)
  waiting for transfers between devices  253 us (33%)
  other arithmetic  114 us (15%)
  matrix products  74.8 us (10%)
  starting transfers between devices  26.4 us (3%)
  loops' own time  14.2 us (2%)
    all_to_all x1, waiting for transfers between devices, per_device(): lax.all_to_all(outgoing, ('gy', 'gz'), split_axis=0, concat_axis=0, tiled...  181 us
    ppermute x15, waiting for transfers between devices, per_device(): main = lax.ppermute(main, ('gy', 'gz'), store)  72.4 us
    unnamed x57, local copies, waits for them, and re-layouts  63.9 us
    dot_general x48, matrix products, contract(): jnp.einsum('anp,bnp->nab', flattened, plane, preferred_element_type=jnp.f...  50.1 us
    convert_element_type x32, other arithmetic, outer(): product_table.reshape((EDGE * EDGE,) + product_table.shape[2:])  29 us
    dynamic_slice x16, local copies, waits for them, and re-layouts, interpolate_advance(): lax.dynamic_slice_in_dim(grid_rows, first_block, batch_blocks, 0)  25.8 us
    gather x1, local copies, waits for them, and re-layouts, per_device(): jnp.take(deposits, source, axis=0)  23.3 us
    dynamic_slice x1, local copies, waits for them, and re-layouts, per_device(): lax.dynamic_slice_in_dim(cell_rows, (step_out ^ ix) * current_arr, curren...  20.2 us
  transfers between devices with their start and end apart: 17, of which 9 were waited for; matrix products, arithmetic and copies ran while one was open for 35% of the time, Pallas kernels for 0%

profile of v1, /device:TPU:13, one launch (start us, length us, event | category | flops | bytes accessed | tf_op | source)
XLA Modules:
  0.0 752.3 jit_solution(17068218777026984747)
XLA Ops:
  5.6 6.5 all-to-all-start
  12.2 2.9 copy.182
  18.1 167.9 %while.23 = (s32[]{:T(128)}, f32[16,4,4,4096]{3,2,1,0:T(4,128)}, s32[16]{0:T(128)S(1)}, f32[16,64,512]{2,1,0:T(8,128)}, s32[]{:T(128)}, /*index=5*/s32[]{:T(128)...) while((s32[]{:T(128)}, f32[16,4,4,4096]{3,2,1,0:T(4,128)}, s32[16]{0:T(128)S(1)}, ...), condition=%wide.region_5.6_spmd, body=%wide.region_4.5_spmd.sunk | while | flops 173355008 | bytes 15483619 | solution.py:124
  185.9 23.3 %gather_fusion.1 = f32[128,4,4096]{2,1,0:T(4,128)} fusion(f32[64,4,4096]{2,1,0:T(4,128)} %bitcast.212, s32[1024]{0:T(1024)S(1)} %pad_clamp_fusion.1), kind=kCustom, calls=%fused_computation.1 | custom fusion | bytes 16777728 | tf_op jit(solution)/shard_map/jit(_take)/gather | solution.py:214
  209.2 11.6 %select_select_fusion = f32[128,4,4096]{2,1,0:T(4,128)} fusion(f32[128,4,4096]{2,1,0:T(4,128)} %gather_fusion.1, pred[128]{0:T(512)(128)(4,1)S(1)} %compare_and_fusion, pred[128]{0:T(512)(128)(4,1)S(1)} %fusion.22), kind=kLoop, calls=%fused_computation.72 | loop fusion | flops 4194304 | bytes 16777472 | tf_op jit(solution)/shard_map/jit(_where)/select_n | solution.py:214
  220.9 6.1 all-to-all-start.1
  228.3 181.0 %all-to-all-done.1 = f32[128,4,4096]{2,1,0:T(4,128)} async-done(((f32[128,4,4096]{2,1,0:T(4,128)}), f32[128,4,4096]{2,1,0:T(4,128)}, u32[]{:S(2)}, u32[]{:S(2)}) %all-to-all-start.1) | async-done | bytes 8388640 | tf_op jit(solution)/shard_map/all_to_all | solution.py:216
  409.4 10.0 %copy.145 = f32[128,4,4096]{0,2,1:T(8,128)} copy(f32[128,4,4096]{2,1,0:T(4,128)} %all-to-all-done.1) | data formatting | bytes 16777216 | tf_op jit(solution)/shard_map/all_to_all | solution.py:216
  419.4 8.1 %fusion.17 = f32[32,4,4096]{2,0,1:T(8,128)S(1)} fusion(f32[128,4,4096]{0,2,1:T(8,128)} %copy.145, f32[128]{0:T(128)S(1)} %eq.54), kind=kOutput, calls=%fused_computation.70 | convolution fusion | flops 805310464 | bytes 10486272 | tf_op jit(solution)/shard_map/dot_general | solution.py:171
  431.7 3.5 copy.147
  435.2 20.2 %constant_dynamic-slice_fusion.5 = (bf16[8,3,4096]{0,2,1:T(8,128)(2,1)}, bf16[8,3,4096]{0,2,1:T(8,128)(2,1)}, bf16[8,3,4096]{0,2,1:T(8,128)(2,1)}, bf16[8,3,4096...) fusion(bf16[128,3,4096]{0,2,1:T(8,128)(2,1)S(1)} %bitcast.199, ...), kind=kLoop, calls=%fused_computation.98 | loop fusion | bytes 6291520 | tf_op jit(solution)/shard_map/dynamic_slice | solution.py:232
  455.4 3.5 copy.164
  458.9 4.0 copy.165
  465.6 4.1 copy.167
  471.8 3.9 copy.168
  479.9 4.0 broadcast_in_dim.121
  487.4 4.1 copy.171
  491.5 4.0 copy.172
  498.1 4.1 copy.174
  502.2 4.0 copy.175
  508.8 4.1 copy.177
  513.0 4.0 copy.178
  538.8 22.0 %collective-permute-done.7 = bf16[8,3,4096]{2,1,0:T(4,128)(2,1)S(1)} collective-permute-done((bf16[8,3,4096]{2,1,0:T(4,128)(2,1)}, bf16[8,3,4096]{2,1,0:T(4,128)(2,1)S(1)}, u32[]{:S(2)}, u32[]{:S(2)}) %collective-permute-start.7) | collective-permute-done | bytes 196640 | tf_op jit(solution)/shard_map/ppermute | solution.py:241
  561.6 10.4 %collective-permute-done.8 = bf16[8,3,4096]{2,1,0:T(4,128)(2,1)S(1)} collective-permute-done((bf16[8,3,4096]{2,1,0:T(4,128)(2,1)}, bf16[8,3,4096]{2,1,0:T(4,128)(2,1)S(1)}, u32[]{:S(2)}, u32[]{:S(2)}) %collective-permute-start.8) | collective-permute-done | bytes 196640 | tf_op jit(solution)/shard_map/ppermute | solution.py:241
  572.9 10.6 %collective-permute-done.9 = bf16[8,3,4096]{2,1,0:T(4,128)(2,1)S(1)} collective-permute-done((bf16[8,3,4096]{2,1,0:T(4,128)(2,1)}, bf16[8,3,4096]{2,1,0:T(4,128)(2,1)S(1)}, u32[]{:S(2)}, u32[]{:S(2)}) %collective-permute-start.9) | collective-permute-done | bytes 196640 | tf_op jit(solution)/shard_map/ppermute | solution.py:241
  585.3 3.7 collective-permute-done.10
  589.9 11.5 %collective-permute-done.11 = bf16[8,3,4096]{2,1,0:T(4,128)(2,1)S(1)} collective-permute-done((bf16[8,3,4096]{2,1,0:T(4,128)(2,1)S(1)}, bf16[8,3,4096]{2,1,0:T(4,128)(2,1)S(1)}, u32[]{:S(2)}, u32[]{:S(2)}) %collective-permute-start.11) | collective-permute-done | bytes 196640 | tf_op jit(solution)/shard_map/ppermute | solution.py:241
  602.2 4.8 collective-permute-done.12
  607.8 4.3 collective-permute-done.13
  612.9 5.0 collective-permute-done.14
  618.7 4.5 gather_fusion.2
  627.0 118.6 %while.24 = (s32[]{:T(128)}, f32[12,64,512]{2,1,0:T(8,128)}, f32[16,64,512]{2,1,0:T(8,128)}, bf16[64,3,4096]{2,1,0:T(4,128)(2,1)}, s32[]{:T(128)}, /*index=5*/s32[]{:T(128)}, s32[]{:T(128)}, s32[]{:T(128)}, s32[]{}) while((s32[]{:T(128)}, f32[12,64,512]{2,1,0:T(8,128)}, f32[16,64,512]{2,1,0:T(8,128)}, bf16[64,3,4096]{2,1,0:T(4,128)(2,1)}, ...), condition=%wide.region_11.12_spmd, body=%wide.region_6.11_spmd.sunk | while | flops 156190720 | bytes 13369515 | solution.py:144
  (811 shorter events, 342.6 us)
Async XLA Ops:
  5.6 215.2 %all-to-all-start = ((f32[16,8,1]{1,2,0:T(1,128)}), f32[16,8,1]{1,2,0:T(1,128)S(1)}, u32[]{:S(2)}, u32[]{:S(2)}) async-start(f32[16,8,1]{1,2,0:T(1,128)} %copy.144), calls=%async_computation | async-start | bytes 16384 | tf_op jit(solution)/shard_map/all_to_all | solution.py:217
  12.2 3.1 copy-start.15
  12.2 3.1 copy-start.8
  12.2 3.1 copy-start.9
  220.9 6.2 copy-start.16
  220.9 188.5 %all-to-all-start.1 = ((f32[128,4,4096]{2,1,0:T(4,128)}), f32[128,4,4096]{2,1,0:T(4,128)}, u32[]{:S(2)}, u32[]{:S(2)}) async-start(f32[128,4,4096]{2,1,0:T(4,128)} %select_select_fusion), calls=%async_computation.1 | async-start | bytes 16777216 | tf_op jit(solution)/shard_map/all_to_all | solution.py:216
  419.4 8.1 %copy-start.11 = (f32[32,4096]{1,0:T(8,128)S(1)}, f32[32,4096]{1,0:T(8,128)}, u32[]{:S(2)}) copy-start(f32[32,4096]{1,0:T(8,128)} %param.21) | copy-start | bytes 1572868
  455.4 7.6 %copy-start.7 = (bf16[8,3,4096]{0,2,1:T(8,128)(2,1)S(1)}, bf16[8,3,4096]{0,2,1:T(8,128)(2,1)}, u32[]{:S(2)}) copy-start(bf16[8,3,4096]{0,2,1:T(8,128)(2,1)} %get-tuple-element.181) | copy-start | bytes 589828
  462.9 56.2 %collective-permute-start = (bf16[8,3,4096]{2,1,0:T(4,128)(2,1)}, bf16[8,3,4096]{2,1,0:T(4,128)(2,1)}, u32[]{:S(2)}, u32[]{:S(2)}) collective-permute-start(bf16[8,3,4096]{2,1,0:T(4,128)(2,1)} %copy.165), channel_id=1, source_target_pairs={{0,1},{1,0},{2,3},{3,2},{4,5},{5,4},{6,7},{7,6},{8,9},{9,8},{10,11... | collective-permute-start | bytes 589832 | tf_op jit(solution)/shard_map/ppermute | solution.py:241
  465.6 55.4 %collective-permute-start.1 = (bf16[8,3,4096]{2,1,0:T(4,128)(2,1)}, bf16[8,3,4096]{2,1,0:T(4,128)(2,1)}, u32[]{:S(2)}, u32[]{:S(2)}) collective-permute-start(bf16[8,3,4096]{2,1,0:T(4,128)(2,1)} %copy.166), channel_id=1, source_target_pairs={{0,2},{1,3},{2,0},{3,1},{4,6},{5,7},{6,4},{7,5},{8,10},{9,11},{10,... | collective-permute-start | bytes 589832 | tf_op jit(solution)/shard_map/ppermute | solution.py:241
  465.6 10.1 %copy-start.6 = (bf16[8,3,4096]{0,2,1:T(8,128)(2,1)S(1)}, bf16[8,3,4096]{0,2,1:T(8,128)(2,1)}, u32[]{:S(2)}) copy-start(bf16[8,3,4096]{0,2,1:T(8,128)(2,1)} %get-tuple-element.178) | copy-start | bytes 589828
  469.8 55.8 %collective-permute-start.2 = (bf16[8,3,4096]{2,1,0:T(4,128)(2,1)}, bf16[8,3,4096]{2,1,0:T(4,128)(2,1)}, u32[]{:S(2)}, u32[]{:S(2)}) collective-permute-start(bf16[8,3,4096]{2,1,0:T(4,128)(2,1)} %copy.167), channel_id=1, source_target_pairs={{0,3},{1,2},{2,1},{3,0},{4,7},{5,6},{6,5},{7,4},{8,11},{9,10},{10,... | collective-permute-start | bytes 589832 | tf_op jit(solution)/shard_map/ppermute | solution.py:241
  475.7 52.7 %collective-permute-start.3 = (bf16[8,3,4096]{2,1,0:T(4,128)(2,1)}, bf16[8,3,4096]{2,1,0:T(4,128)(2,1)}, u32[]{:S(2)}, u32[]{:S(2)}) collective-permute-start(bf16[8,3,4096]{2,1,0:T(4,128)(2,1)} %copy.168), channel_id=1, source_target_pairs={{0,4},{1,5},{2,6},{3,7},{4,0},{5,1},{6,2},{7,3},{8,12},{9,13},{10,... | collective-permute-start | bytes 589832 | tf_op jit(solution)/shard_map/ppermute | solution.py:241
  478.6 6.1 copy-start.5
  478.6 52.8 %collective-permute-start.4 = (bf16[8,3,4096]{2,1,0:T(4,128)(2,1)}, bf16[8,3,4096]{2,1,0:T(4,128)(2,1)}, u32[]{:S(2)}, u32[]{:S(2)}) collective-permute-start(bf16[8,3,4096]{2,1,0:T(4,128)(2,1)} %copy.169), channel_id=1, source_target_pairs={{0,5},{1,4},{2,7},{3,6},{4,1},{5,0},{6,3},{7,2},{8,13},{9,12},{10,... | collective-permute-start | bytes 589832 | tf_op jit(solution)/shard_map/ppermute | solution.py:241
  487.4 8.1 %copy-start.4 = (bf16[8,3,4096]{0,2,1:T(8,128)(2,1)S(1)}, bf16[8,3,4096]{0,2,1:T(8,128)(2,1)}, u32[]{:S(2)}) copy-start(bf16[8,3,4096]{0,2,1:T(8,128)(2,1)} %get-tuple-element.174) | copy-start | bytes 589828
  498.1 8.1 %copy-start.3 = (bf16[8,3,4096]{0,2,1:T(8,128)(2,1)S(1)}, bf16[8,3,4096]{0,2,1:T(8,128)(2,1)}, u32[]{:S(2)}) copy-start(bf16[8,3,4096]{0,2,1:T(8,128)(2,1)} %get-tuple-element.171) | copy-start | bytes 589828
  508.8 8.1 %copy-start.2 = (bf16[8,3,4096]{0,2,1:T(8,128)(2,1)S(1)}, bf16[8,3,4096]{0,2,1:T(8,128)(2,1)}, u32[]{:S(2)}) copy-start(bf16[8,3,4096]{0,2,1:T(8,128)(2,1)} %get-tuple-element.168) | copy-start | bytes 589828
  519.0 18.8 %copy-start.14 = (bf16[8,3,4096]{2,1,0:T(4,128)(2,1)S(1)}, bf16[8,3,4096]{2,1,0:T(4,128)(2,1)}, u32[]{:S(2)}) copy-start(bf16[8,3,4096]{2,1,0:T(4,128)(2,1)} %copy.176) | copy-start | bytes 589828
  519.0 41.8 %copy-start.13 = (bf16[8,3,4096]{2,1,0:T(4,128)(2,1)S(1)}, bf16[8,3,4096]{2,1,0:T(4,128)(2,1)}, u32[]{:S(2)}) copy-start(bf16[8,3,4096]{2,1,0:T(4,128)(2,1)} %copy.177) | copy-start | bytes 589828
  519.1 53.0 %copy-start.12 = (bf16[8,3,4096]{2,1,0:T(4,128)(2,1)S(1)}, bf16[8,3,4096]{2,1,0:T(4,128)(2,1)}, u32[]{:S(2)}) copy-start(bf16[8,3,4096]{2,1,0:T(4,128)(2,1)} %copy.178) | copy-start | bytes 589828
  519.1 15.4 %collective-permute-start.5 = (bf16[8,3,4096]{2,1,0:T(4,128)(2,1)}, bf16[8,3,4096]{2,1,0:T(4,128)(2,1)S(1)}, u32[]{:S(2)}, u32[]{:S(2)}) collective-permute-start(bf16[8,3,4096]{2,1,0:T(4,128)(2,1)} %copy.170), channel_id=1, source_target_pairs={{0,6},{1,7},{2,4},{3,5},{4,2},{5,3},{6,0},{7,1},{8,14},{9,15},{10,... | collective-permute-start | bytes 589832 | tf_op jit(solution)/shard_map/ppermute | solution.py:241
  521.0 16.9 %collective-permute-start.6 = (bf16[8,3,4096]{2,1,0:T(4,128)(2,1)}, bf16[8,3,4096]{2,1,0:T(4,128)(2,1)S(1)}, u32[]{:S(2)}, u32[]{:S(2)}) collective-permute-start(bf16[8,3,4096]{2,1,0:T(4,128)(2,1)} %copy.171), channel_id=1, source_target_pairs={{0,7},{1,6},{2,5},{3,4},{4,3},{5,2},{6,1},{7,0},{8,15},{9,14},{10,... | collective-permute-start | bytes 589832 | tf_op jit(solution)/shard_map/ppermute | solution.py:241
  525.6 35.2 %collective-permute-start.7 = (bf16[8,3,4096]{2,1,0:T(4,128)(2,1)}, bf16[8,3,4096]{2,1,0:T(4,128)(2,1)S(1)}, u32[]{:S(2)}, u32[]{:S(2)}) collective-permute-start(bf16[8,3,4096]{2,1,0:T(4,128)(2,1)} %copy.172), channel_id=1, source_target_pairs={{0,8},{1,9},{2,10},{3,11},{4,12},{5,13},{6,14},{7,15},{8,0},{9,1},... | collective-permute-start | bytes 589832 | tf_op jit(solution)/shard_map/ppermute | solution.py:241
  528.4 43.6 %collective-permute-start.8 = (bf16[8,3,4096]{2,1,0:T(4,128)(2,1)}, bf16[8,3,4096]{2,1,0:T(4,128)(2,1)S(1)}, u32[]{:S(2)}, u32[]{:S(2)}) collective-permute-start(bf16[8,3,4096]{2,1,0:T(4,128)(2,1)} %copy.173), channel_id=1, source_target_pairs={{0,9},{1,8},{2,11},{3,10},{4,13},{5,12},{6,15},{7,14},{8,1},{9,0},... | collective-permute-start | bytes 589832 | tf_op jit(solution)/shard_map/ppermute | solution.py:241
  531.4 52.0 %collective-permute-start.9 = (bf16[8,3,4096]{2,1,0:T(4,128)(2,1)}, bf16[8,3,4096]{2,1,0:T(4,128)(2,1)S(1)}, u32[]{:S(2)}, u32[]{:S(2)}) collective-permute-start(bf16[8,3,4096]{2,1,0:T(4,128)(2,1)} %copy.174), channel_id=1, source_target_pairs={{0,10},{1,11},{2,8},{3,9},{4,14},{5,15},{6,12},{7,13},{8,2},{9,3},... | collective-permute-start | bytes 589832 | tf_op jit(solution)/shard_map/ppermute | solution.py:241
  534.5 54.6 %collective-permute-start.10 = (bf16[8,3,4096]{2,1,0:T(4,128)(2,1)}, bf16[8,3,4096]{2,1,0:T(4,128)(2,1)S(1)}, u32[]{:S(2)}, u32[]{:S(2)}) collective-permute-start(bf16[8,3,4096]{2,1,0:T(4,128)(2,1)} %copy.175), channel_id=1, source_target_pairs={{0,11},{1,10},{2,9},{3,8},{4,15},{5,14},{6,13},{7,12},{8,3},{9,2},... | collective-permute-start | bytes 589832 | tf_op jit(solution)/shard_map/ppermute | solution.py:241
  537.9 63.5 %collective-permute-start.11 = (bf16[8,3,4096]{2,1,0:T(4,128)(2,1)S(1)}, bf16[8,3,4096]{2,1,0:T(4,128)(2,1)S(1)}, u32[]{:S(2)}, u32[]{:S(2)}) collective-permute-start(bf16[8,3,4096]{2,1,0:T(4,128)(2,1)S(1)} %copy-done.14), channel_id=1, source_target_pairs={{0,12},{1,13},{2,14},{3,15},{4,8},{5,9},{6,10},{7,11},{8,4},{9,5},... | collective-permute-start | bytes 589832 | tf_op jit(solution)/shard_map/ppermute | solution.py:241
  560.8 46.2 %collective-permute-start.12 = (bf16[8,3,4096]{2,1,0:T(4,128)(2,1)S(1)}, bf16[8,3,4096]{2,1,0:T(4,128)(2,1)S(1)}, u32[]{:S(2)}, u32[]{:S(2)}) collective-permute-start(bf16[8,3,4096]{2,1,0:T(4,128)(2,1)S(1)} %copy-done.13), channel_id=1, source_target_pairs={{0,13},{1,12},{2,15},{3,14},{4,9},{5,8},{6,11},{7,10},{8,5},{9,4},... | collective-permute-start | bytes 589832 | tf_op jit(solution)/shard_map/ppermute | solution.py:241
  572.1 40.1 %collective-permute-start.13 = (bf16[8,3,4096]{2,1,0:T(4,128)(2,1)S(1)}, bf16[8,3,4096]{2,1,0:T(4,128)(2,1)S(1)}, u32[]{:S(2)}, u32[]{:S(2)}) collective-permute-start(bf16[8,3,4096]{2,1,0:T(4,128)(2,1)S(1)} %copy-done.12), channel_id=1, source_target_pairs={{0,14},{1,15},{2,12},{3,13},{4,10},{5,11},{6,8},{7,9},{8,6},{9,7},... | collective-permute-start | bytes 589832 | tf_op jit(solution)/shard_map/ppermute | solution.py:241
  583.4 34.5 %collective-permute-start.14 = (bf16[8,3,4096]{2,1,0:T(4,128)(2,1)S(1)}, bf16[8,3,4096]{2,1,0:T(4,128)(2,1)S(1)}, u32[]{:S(2)}, u32[]{:S(2)}) collective-permute-start(bf16[8,3,4096]{2,1,0:T(4,128)(2,1)S(1)} %copy.179), channel_id=1, source_target_pairs={{0,15},{1,14},{2,13},{3,12},{4,11},{5,10},{6,9},{7,8},{8,7},{9,6},... | collective-permute-start | bytes 589832 | tf_op jit(solution)/shard_map/ppermute | solution.py:241
  748.0 3.9 copy-start.1
  (3 other events, 5.0 us)
